TPU v7x, 32 devices: a 4x2x2 block of a 4x4x8 slice. The times are simulated.
32 devices in a mesh: mat: 4 (over y, z), dp: 8 (over x, core).
Axes of the slice: x: 4, y: 2, z: 2, core: 2. Of those that a mesh axis runs over, the one named last changes fastest.
The devices are a block of a 4x4x8 slice.
Arguments:
- a_mat: bfloat16 [14336, 32768], P('mat', 'dp'), parts along dimension 0
Outputs:
- output: float32 [32, 5, 448, 448], P(('mat', 'dp')), parts along dimension 0
There are 4 independent parts. A program takes and returns all parts, laid end to end along the dimension named above; each array names one.
All inputs are finite; a program needn't handle non-finite values.
Results may differ from a plain program's by a relative error of at most 0.001.
Values are sent between devices in bfloat16 or wider.
A program may use at most 768 MiB of HBM per device.

v0:
```python
import jax
import jax.numpy as jnp
from jax import lax
from jax.sharding import PartitionSpec as P


def packed_partial(blocks):
    groups = blocks.shape[0]
    blk_rows = blocks.shape[1]
    half = groups // 2
    slots = half + 1
    doubled = jnp.concatenate([blocks, blocks], axis=0)
    dev_ids = lax.broadcasted_iota(jnp.int32, (groups, 1, 1), 0)

    def slot_step(slot, packed):
        partner = lax.dynamic_slice_in_dim(doubled, groups - slot, groups, axis=0)
        block_prod = jnp.einsum('gik,gjk->gij', blocks, partner, preferred_element_type=jnp.float32)
        flipped = jnp.where(dev_ids < slot, jnp.swapaxes(block_prod, 1, 2), block_prod)
        keep_mask = jnp.logical_or(slot < half, dev_ids < half)
        return lax.dynamic_update_index_in_dim(packed, jnp.where(keep_mask, flipped, 0.0), slot, axis=1)

    packed = jnp.zeros((groups, slots, blk_rows, blk_rows), jnp.float32)
    return lax.fori_loop(0, slots, slot_step, packed)


def solution(mesh):
    groups = mesh.shape['dp']

    def local_gram(a_local):
        n_rows, local_cols = a_local.shape
        blocks = a_local.reshape(groups, n_rows // groups, local_cols)
        return lax.psum_scatter(packed_partial(blocks), 'dp', scatter_dimension=0, tiled=True)

    return jax.shard_map(local_gram, mesh=mesh, in_specs=(P('mat', 'dp'),), out_specs=P(('mat', 'dp')), check_vma=False)
```

profile of v0, /device:TPU:81, one launch (start us, length us, event | category | flops | bytes accessed | tf_op | source)
XLA Modules:
  0.0 460.2 jit_solution(8886043612065403474)
XLA Ops:
  6.5 0.0 reduce-scatter.2.cloned.1.call-start
  6.6 38.9 %pad_maximum_fusion = bf16[16,448,4096]{2,1,0:T(8,128)(2,1)} fusion(bf16[8,448,4096]{2,1,0:T(8,128)(2,1)} %bitcast.24), kind=kLoop, calls=%fused_computation.9 | loop fusion | flops 29360128 | bytes 88080384 | tf_op jit(solution)/shard_map/concatenate | solution.py:12
  45.4 221.9 %while.17 = (s32[]{:T(128)}, f32[8,5,448,448]{3,2,1,0:T(8,128)}, bf16[16,448,4096]{2,1,0:T(8,128)(2,1)}, bf16[8,448,4096]{2,1,0:T(8,128)(2,1)}, s32[]{:T(128)}, ...) while((s32[]{:T(128)}, f32[8,5,448,448]{3,2,1,0:T(8,128)}, ...), condition=%wide.region_1.2_spmd.clone.clone, body=%wide.region_0.1_spmd.clone.clone.sunk | while | flops 13156548608 | bytes 100008640 | solution.py:23
  45.4 25.8 %fusion.12 = f32[8,448,448]{2,1,0:T(8,128)} fusion(bf16[8,448,4096]{2,1,0:T(8,128)(2,1)} %get-tuple-element.225, bf16[16,448,4096]{2,1,0:T(8,128)(2,1)} %get-tuple-element.224, s32[]{:T(128)S(6)} %select_n.60), kind=kOutput, calls=%fused_computation.1.clone.1 | convolution fusion | flops 13153337344 | bytes 65142788 | tf_op jit(solution)/shard_map/while/body/eval_jaxpr/gik,gjk->gij/dot_general | solution.py:17
  71.2 8.5 %copy.7 = f32[8,448,448]{1,2,0:T(8,128)} copy(f32[8,448,448]{2,1,0:T(8,128)} %fusion.12) | data formatting | bytes 12845056 | tf_op jit(solution)/shard_map/while/body/eval_jaxpr/gik,gjk->gij/dot_general | solution.py:17
  79.8 10.0 %bitcast_dynamic-update-slice_fusion.2 = f32[8,5,448,448]{3,2,1,0:T(8,128)} fusion(f32[8,5,448,448]{3,2,1,0:T(8,128)} %get-tuple-element.214, s32[]{:T(128)} %get-tuple-element.213, f32[8,448,448]{2,1,0:T(8,128)} %fusion.12, f32[8,448,448]{1,2,0:T(8,128)} %copy.7, pred[8]{0:T(512)(128)(4,1)S(1)} %get-tuple-element.202, ...), kind=kLoop, calls=%fused_computation.3.clone.1 | loop fusion | flops 3211264 | bytes 22020624 | tf_op jit(solution)/shard_map/while/body/eval_jaxpr/jit(dynamic_update_index_in_dim)/dynamic_update_slice | solution.py:20
  89.8 25.8 %fusion.12 = f32[8,448,448]{2,1,0:T(8,128)} fusion(bf16[8,448,4096]{2,1,0:T(8,128)(2,1)} %get-tuple-element.225, bf16[16,448,4096]{2,1,0:T(8,128)(2,1)} %get-tuple-element.224, s32[]{:T(128)S(6)} %select_n.60), kind=kOutput, calls=%fused_computation.1.clone.1 | convolution fusion | flops 13153337344 | bytes 65142788 | tf_op jit(solution)/shard_map/while/body/eval_jaxpr/gik,gjk->gij/dot_general | solution.py:17
  115.6 8.5 %copy.7 = f32[8,448,448]{1,2,0:T(8,128)} copy(f32[8,448,448]{2,1,0:T(8,128)} %fusion.12) | data formatting | bytes 12845056 | tf_op jit(solution)/shard_map/while/body/eval_jaxpr/gik,gjk->gij/dot_general | solution.py:17
  124.1 10.0 %bitcast_dynamic-update-slice_fusion.2 = f32[8,5,448,448]{3,2,1,0:T(8,128)} fusion(f32[8,5,448,448]{3,2,1,0:T(8,128)} %get-tuple-element.214, s32[]{:T(128)} %get-tuple-element.213, f32[8,448,448]{2,1,0:T(8,128)} %fusion.12, f32[8,448,448]{1,2,0:T(8,128)} %copy.7, pred[8]{0:T(512)(128)(4,1)S(1)} %get-tuple-element.202, ...), kind=kLoop, calls=%fused_computation.3.clone.1 | loop fusion | flops 3211264 | bytes 22020624 | tf_op jit(solution)/shard_map/while/body/eval_jaxpr/jit(dynamic_update_index_in_dim)/dynamic_update_slice | solution.py:20
  134.1 25.8 %fusion.12 = f32[8,448,448]{2,1,0:T(8,128)} fusion(bf16[8,448,4096]{2,1,0:T(8,128)(2,1)} %get-tuple-element.225, bf16[16,448,4096]{2,1,0:T(8,128)(2,1)} %get-tuple-element.224, s32[]{:T(128)S(6)} %select_n.60), kind=kOutput, calls=%fused_computation.1.clone.1 | convolution fusion | flops 13153337344 | bytes 65142788 | tf_op jit(solution)/shard_map/while/body/eval_jaxpr/gik,gjk->gij/dot_general | solution.py:17
  159.9 8.5 %copy.7 = f32[8,448,448]{1,2,0:T(8,128)} copy(f32[8,448,448]{2,1,0:T(8,128)} %fusion.12) | data formatting | bytes 12845056 | tf_op jit(solution)/shard_map/while/body/eval_jaxpr/gik,gjk->gij/dot_general | solution.py:17
  168.4 10.1 %bitcast_dynamic-update-slice_fusion.2 = f32[8,5,448,448]{3,2,1,0:T(8,128)} fusion(f32[8,5,448,448]{3,2,1,0:T(8,128)} %get-tuple-element.214, s32[]{:T(128)} %get-tuple-element.213, f32[8,448,448]{2,1,0:T(8,128)} %fusion.12, f32[8,448,448]{1,2,0:T(8,128)} %copy.7, pred[8]{0:T(512)(128)(4,1)S(1)} %get-tuple-element.202, ...), kind=kLoop, calls=%fused_computation.3.clone.1 | loop fusion | flops 3211264 | bytes 22020624 | tf_op jit(solution)/shard_map/while/body/eval_jaxpr/jit(dynamic_update_index_in_dim)/dynamic_update_slice | solution.py:20
  178.5 25.8 %fusion.12 = f32[8,448,448]{2,1,0:T(8,128)} fusion(bf16[8,448,4096]{2,1,0:T(8,128)(2,1)} %get-tuple-element.225, bf16[16,448,4096]{2,1,0:T(8,128)(2,1)} %get-tuple-element.224, s32[]{:T(128)S(6)} %select_n.60), kind=kOutput, calls=%fused_computation.1.clone.1 | convolution fusion | flops 13153337344 | bytes 65142788 | tf_op jit(solution)/shard_map/while/body/eval_jaxpr/gik,gjk->gij/dot_general | solution.py:17
  204.3 8.5 %copy.7 = f32[8,448,448]{1,2,0:T(8,128)} copy(f32[8,448,448]{2,1,0:T(8,128)} %fusion.12) | data formatting | bytes 12845056 | tf_op jit(solution)/shard_map/while/body/eval_jaxpr/gik,gjk->gij/dot_general | solution.py:17
  212.8 10.1 %bitcast_dynamic-update-slice_fusion.2 = f32[8,5,448,448]{3,2,1,0:T(8,128)} fusion(f32[8,5,448,448]{3,2,1,0:T(8,128)} %get-tuple-element.214, s32[]{:T(128)} %get-tuple-element.213, f32[8,448,448]{2,1,0:T(8,128)} %fusion.12, f32[8,448,448]{1,2,0:T(8,128)} %copy.7, pred[8]{0:T(512)(128)(4,1)S(1)} %get-tuple-element.202, ...), kind=kLoop, calls=%fused_computation.3.clone.1 | loop fusion | flops 3211264 | bytes 22020624 | tf_op jit(solution)/shard_map/while/body/eval_jaxpr/jit(dynamic_update_index_in_dim)/dynamic_update_slice | solution.py:20
  222.9 25.8 %fusion.12 = f32[8,448,448]{2,1,0:T(8,128)} fusion(bf16[8,448,4096]{2,1,0:T(8,128)(2,1)} %get-tuple-element.225, bf16[16,448,4096]{2,1,0:T(8,128)(2,1)} %get-tuple-element.224, s32[]{:T(128)S(6)} %select_n.60), kind=kOutput, calls=%fused_computation.1.clone.1 | convolution fusion | flops 13153337344 | bytes 65142788 | tf_op jit(solution)/shard_map/while/body/eval_jaxpr/gik,gjk->gij/dot_general | solution.py:17
  248.7 8.5 %copy.7 = f32[8,448,448]{1,2,0:T(8,128)} copy(f32[8,448,448]{2,1,0:T(8,128)} %fusion.12) | data formatting | bytes 12845056 | tf_op jit(solution)/shard_map/while/body/eval_jaxpr/gik,gjk->gij/dot_general | solution.py:17
  257.2 10.1 %bitcast_dynamic-update-slice_fusion.2 = f32[8,5,448,448]{3,2,1,0:T(8,128)} fusion(f32[8,5,448,448]{3,2,1,0:T(8,128)} %get-tuple-element.214, s32[]{:T(128)} %get-tuple-element.213, f32[8,448,448]{2,1,0:T(8,128)} %fusion.12, f32[8,448,448]{1,2,0:T(8,128)} %copy.7, pred[8]{0:T(512)(128)(4,1)S(1)} %get-tuple-element.202, ...), kind=kLoop, calls=%fused_computation.3.clone.1 | loop fusion | flops 3211264 | bytes 22020624 | tf_op jit(solution)/shard_map/while/body/eval_jaxpr/jit(dynamic_update_index_in_dim)/dynamic_update_slice | solution.py:20
  267.3 0.1 reduce-scatter.2.cloned.1.call-update
  267.3 186.0 %reduce-scatter.2.cloned.1.call-done = f32[1,5,448,448]{3,2,1,0:T(8,128)} async-done(((f32[8,5,448,448]{3,2,1,0:T(8,128)}), f32[1,5,448,448]{3,2,1,0:T(8,128)}) %reduce-scatter.2.cloned.1.call-update) | async-done | bytes 4014096 | tf_op jit(solution)/shard_map/reduce_scatter | solution.py:32
  (6 shorter events, 0.0 us)
Async XLA Ops:
  6.5 446.8 %reduce-scatter.2.cloned.1.call-start = ((), (), s32[]{:S(2)}) async-start(), calls=%async_computation.1 | async-start | bytes 41287680 | tf_op jit(solution)/shard_map/reduce_scatter | solution.py:32
Sparse Core Ops, SparseCore 0:
  267.5 185.8 reduce-scatter.1
where the time goes:
time: 461 us; the launch traced here: 460 us
  waiting for transfers between devices  186 us (40%)
  matrix products  129 us (28%)
  other arithmetic  89.1 us (19%)
  local copies, waits for them, and re-layouts  42.6 us (9%)
  between operations  13.4 us (3%)
    reduce_scatter x1, waiting for transfers between devices, local_gram(): lax.psum_scatter(packed_partial(blocks), 'dp', scatter_dimension=0, tiled...  186 us
    dot_general x5, matrix products, slot_step(): jnp.einsum('gik,gjk->gij', blocks, partner, preferred_element_type=jnp.fl...  129 us
    dynamic_update_slice x5, other arithmetic, slot_step(): lax.dynamic_update_index_in_dim(packed, jnp.where(keep_mask, flipped, 0.0...  50.2 us
    dot_general x5, local copies, waits for them, and re-layouts, slot_step(): jnp.einsum('gik,gjk->gij', blocks, partner, preferred_element_type=jnp.fl...  42.6 us
    concatenate x1, other arithmetic, packed_partial(): doubled = jnp.concatenate([blocks, blocks], axis=0)  38.9 us
  transfers between devices with their start and end apart: 1, of which 1 were waited for; matrix products, arithmetic and copies ran while one was open for 0% of the time, Pallas kernels for 0%

commit v1 on v0

v1 whole, which is shorter than its diff:
```python
import functools

import jax
import jax.numpy as jnp
from jax import lax
from jax.experimental import pallas as pl
from jax.experimental.pallas import tpu as pltpu
from jax.sharding import PartitionSpec as P

CORES = 2
LANES = 128
O_SLOTS = 4
MESH = pl.DeviceIdType.MESH


def _kernel(groups, blk, a_hbm, out_hbm, a, x, ring, outgoing, acc, stage,
            load_sem, pair_send, pair_recv, ring_send, ring_recv, out_sem):
    chips = groups // CORES
    half_groups = groups // 2
    slots = half_groups + 1
    steps = chips - 1
    per_step = 2 * slots
    n_items = chips * per_step
    wide = 2 * LANES
    mid = blk // 2
    rows_l, rows_s = 2 * blk, blk + mid
    edge = blk - LANES
    low = blk - wide
    rows_dl, rows_ds = 2 * blk - LANES, LANES + low // 2
    blk_rows = rows_l + rows_s
    ring_rows = half_groups // 2 * blk_rows + rows_l
    tail = edge - wide

    me = lax.axis_index("dp")
    chip, core = me // CORES, me % CORES
    partner = chip * CORES + 1 - core
    chip_up = (chip + 1) % chips
    chip_down = (chip + chips - 1) % chips
    up, down = chip_up * CORES + core, chip_down * CORES + core

    def row_block(index):
        return pl.ds(pl.multiple_of(index * blk, 64), blk)

    def load(index):
        return pltpu.make_async_copy(a_hbm.at[row_block(index)], a.at[row_block(index)], load_sem.at[index])

    first = (chip_down * CORES + 1 - core, chip_up * CORES + 1 - core, chip_down * CORES + core, chip_up * CORES + core)
    chip_far = (chip + 2) % chips
    rest = (chip * CORES + 1 - core, chip * CORES + core, chip_far * CORES + 1 - core, chip_far * CORES + core)
    for index in first + rest:
        load(index).start()

    barrier = pltpu.get_barrier_semaphore()
    for other in (partner, up, down):
        pl.semaphore_signal(barrier, inc=1, device_id={"dp": other}, device_id_type=MESH)
    pl.semaphore_wait(barrier, 3)

    def item(n):
        step = n // per_step
        rest_n = n % per_step
        slot, way = rest_n // 2, rest_n % 2
        dest = (chip + 2 * chips + (1 + step) * (2 * way - 1)) % chips
        valid = jnp.logical_or(slot < half_groups, dest < chips // 2)
        return step, slot, way, dest, (slot + way) % 2, valid

    def by_case(slot, half, fn):
        for diag in (True, False):
            for part in (0, 1):
                cond = jnp.logical_and((slot == 0) if diag else (slot > 0), half == part)
                rows = ((rows_dl, rows_ds) if diag else (rows_l, rows_s))[part]
                pl.when(cond)(functools.partial(fn, diag, part, rows))

    def multiply(dest, parity, slot, half):
        p = dest * CORES + parity
        q = (p - slot + groups) % groups
        wrapped = (slot + groups - 1 - p) // groups
        hi = p + wrapped * (q - p)
        lo = q + wrapped * (p - q)
        left = a[row_block(hi), :]
        right = a[pl.ds(pl.multiple_of(lo * blk + half * (blk - wide), 64), wide), :]
        acc[...] = lax.dot_general(left, right, (((1,), (1,)), ((), ())), preferred_element_type=jnp.float32)

    def emit(diag, part, put):
        if part == 0:
            skip = LANES if diag else 0
            put(0, acc[:, :LANES])
            put(blk, acc[skip:, LANES:])
        else:
            top = wide if diag else 0
            cut = (top + blk) // 2
            put(0, acc[edge if diag else 0:, LANES:])
            lane = lax.broadcasted_iota(jnp.int32, (blk - cut, LANES), 1)
            put(LANES if diag else blk, jnp.where(lane < tail, pltpu.roll(acc[top:cut, :LANES], tail, 1), acc[cut:, :LANES]))

    def x_base(dest, slot, half):
        return pl.multiple_of((dest * slots + slot) * blk_rows + half * rows_l, 32)

    def ring_base(step, slot, way):
        off = (slot // 2) * blk_rows + (slot % 2) * (rows_l + way * (rows_s - rows_l))
        return pl.multiple_of((way * steps + step) * ring_rows + off, 32)

    def pair_copy(n, dest, slot, half, rows):
        return pltpu.make_async_remote_copy(
            src_ref=outgoing.at[pl.ds(pl.multiple_of((n % O_SLOTS) * rows_l, 32), rows)],
            dst_ref=x.at[pl.ds(x_base(dest, slot, half), rows)],
            send_sem=pair_send.at[n], recv_sem=pair_recv.at[n],
            device_id={"dp": partner}, device_id_type=MESH)

    def ring_copy(step, slot, way, dest, half, rows):
        target = up + way * (down - up)
        sem = (way * steps + step) * slots + slot
        return pltpu.make_async_remote_copy(
            src_ref=x.at[pl.ds(x_base(dest, slot, half), rows)],
            dst_ref=ring.at[pl.ds(ring_base(step, slot, way), rows)],
            send_sem=ring_send.at[sem], recv_sem=ring_recv.at[sem],
            device_id={"dp": target}, device_id_type=MESH)

    def wait_pair_send(n):
        _, slot, _, dest, half, valid = item(n)

        @pl.when(valid)
        def _():
            by_case(slot, half, lambda diag, part, rows: pair_copy(n, dest, slot, half, rows).wait_send())

    def for_partner(n):
        _, slot, _, dest, half, valid = item(n)

        @pl.when(n >= O_SLOTS)
        def _():
            wait_pair_send(n - O_SLOTS)

        @pl.when(valid)
        def _():
            multiply(dest, 1 - core, slot, half)
            base = (n % O_SLOTS) * rows_l

            def send(diag, part, rows):
                def put(row, value):
                    outgoing[pl.ds(pl.multiple_of(base + row, 32), value.shape[0]), :] = value

                emit(diag, part, put)
                pair_copy(n, dest, slot, half, rows).start()

            by_case(slot, half, send)

    def out_copy(slot):
        return pltpu.make_async_copy(stage.at[slot % 2], out_hbm.at[slot], out_sem.at[slot % 2])

    def finish(slot, diag, part, value):
        block = stage.at[slot % 2]
        if part == 0 and not diag:
            block[:, :LANES] = value(0, blk)
            block[:, LANES:wide] = value(blk, blk)
        elif part == 0:
            col0 = value(0, blk)
            col1 = value(blk, blk - LANES)
            block[:, :LANES] = col0
            block[LANES:, LANES:wide] = col1
            block[:LANES, LANES:wide] = col0[LANES:wide].T
            block[:LANES, wide:3 * LANES] = col0[wide:3 * LANES].T
            block[:LANES, 3 * LANES:] = col0[3 * LANES:].T
            block[LANES:wide, wide:3 * LANES] = col1[LANES:wide].T
            block[LANES:wide, 3 * LANES:] = col1[wide:].T
        else:
            top = wide if diag else 0
            cut = (blk - top) // 2
            tile = value(0, LANES if diag else blk)
            strip = value(LANES if diag else blk, cut)
            rolled = pltpu.roll(strip, tail, 1)
            if diag:
                across = jnp.concatenate([strip[tail:], rolled], axis=0)[:, :tail].T
                tile = jnp.concatenate([across, tile], axis=0)
            tile = pltpu.roll(tile, tail, 1)
            lane = lax.broadcasted_iota(jnp.int32, (cut, LANES), 1)
            block[top:top + cut, wide:3 * LANES] = jnp.where(lane < tail, strip, tile[:cut])
            block[top + cut:, wide:3 * LANES] = jnp.where(lane < tail, rolled, tile[cut:])
            block[top:, 3 * LANES:] = tile[:, :tail]

    def for_me(n):
        step, slot, way, dest, half, valid = item(n)

        @pl.when(valid)
        def _():
            multiply(dest, core, slot, half)
            base = x_base(dest, slot, half)

            def add(diag, part, rows):
                pair_copy(n, dest, slot, half, rows).wait_recv()

                def put(row, value):
                    span = pl.ds(pl.multiple_of(base + row, 32), value.shape[0])
                    x[span, :] = x[span, :] + value

                emit(diag, part, put)

                @pl.when(step > 0)
                def _():
                    ring_copy(step - 1, slot, way, dest, half, rows).wait_recv()

                r_base = ring_base(step - 1, slot, way)

                def value(row, size):
                    return (x[pl.ds(pl.multiple_of(base + row, 32), size), :]
                            + ring[pl.ds(pl.multiple_of(r_base + row, 32), size), :])

                @pl.when(jnp.logical_and(step > 0, step < steps))
                def _():
                    x[pl.ds(base, rows), :] = value(0, rows)

                @pl.when(step < steps)
                def _():
                    ring_copy(step, slot, way, dest, half, rows).start()

                @pl.when(step == steps)
                def _():
                    finish(slot, diag, part, value)

            @pl.when(jnp.logical_and(step == steps, jnp.logical_and(way == 0, slot >= 2)))
            def _():
                out_copy(slot - 2).wait()

            by_case(slot, half, add)

        @pl.when(jnp.logical_and(step == steps, jnp.logical_not(valid)))
        def _():
            @pl.when(way == 0)
            def _():
                out_copy(slot - 2).wait()
                stage[slot % 2] = jnp.zeros(stage.shape[1:], stage.dtype)

        @pl.when(jnp.logical_and(step == steps, way == 1))
        def _():
            out_copy(slot).start()

    load(first[0]).wait()
    for_partner(0)

    def body(n, carry):
        @pl.when(n == 0)
        def _():
            load(first[1]).wait()

        @pl.when(n == 1)
        def _():
            load(first[3]).wait()
            for index in rest:
                load(index).wait()

        @pl.when(n + 1 < n_items)
        def _():
            for_partner(n + 1)

        @pl.when(n == 0)
        def _():
            load(first[2]).wait()

        for_me(n)
        return carry

    lax.fori_loop(0, n_items, body, 0)

    def drain(n, carry):
        step, slot, way, dest, half, valid = item(n)

        @pl.when(valid)
        def _():
            by_case(slot, half, lambda diag, part, rows: ring_copy(step, slot, way, dest, half, rows).wait_send())

        return carry

    lax.fori_loop(0, steps * per_step, drain, 0)
    for n in range(n_items - O_SLOTS, n_items):
        wait_pair_send(n)
    for slot in (slots - 2, slots - 1):
        out_copy(slot).wait()


def solution(mesh):
    groups = mesh.shape["dp"]
    chips = groups // CORES
    slots = groups // 2 + 1

    def local_gram(a_local):
        n_rows, local_cols = a_local.shape
        blk = n_rows // groups
        rows_l, rows_s = 2 * blk, blk + blk // 2
        blk_rows = rows_l + rows_s
        ring_rows = groups // 4 * blk_rows + rows_l
        n_items = chips * 2 * slots
        n_ring = 2 * (chips - 1) * slots
        return pl.pallas_call(
            functools.partial(_kernel, groups, blk),
            out_shape=jax.ShapeDtypeStruct((slots, blk, blk), jnp.float32),
            in_specs=[pl.BlockSpec(memory_space=pl.ANY)],
            out_specs=pl.BlockSpec(memory_space=pl.ANY),
            scratch_shapes=[
                pltpu.VMEM((n_rows, local_cols), jnp.bfloat16),
                pltpu.VMEM((chips * slots * blk_rows, LANES), jnp.float32),
                pltpu.VMEM((2 * (chips - 1) * ring_rows, LANES), jnp.float32),
                pltpu.VMEM((O_SLOTS * rows_l, LANES), jnp.float32),
                pltpu.VMEM((blk, 2 * LANES), jnp.float32),
                pltpu.VMEM((2, blk, blk), jnp.float32),
                pltpu.SemaphoreType.DMA((groups,)),
                pltpu.SemaphoreType.DMA((n_items,)),
                pltpu.SemaphoreType.DMA((n_items,)),
                pltpu.SemaphoreType.DMA((n_ring,)),
                pltpu.SemaphoreType.DMA((n_ring,)),
                pltpu.SemaphoreType.DMA((2,)),
            ],
            compiler_params=pltpu.CompilerParams(
                collective_id=0, has_side_effects=True, vmem_limit_bytes=67_043_328),
        )(a_local)[None]

    return jax.shard_map(local_gram, mesh=mesh, in_specs=(P("mat", "dp"),), out_specs=P(("mat", "dp")), check_vma=False)
```

time: 461 us -> 139 us (0.30)
  waiting for transfers between devices: 186 us -> 0 us
  Pallas kernels: 0 us -> 133 us
  matrix products: 129 us -> 0 us
  other arithmetic: 89.1 us -> 0 us
  local copies, waits for them, and re-layouts: 42.6 us -> 5.26 us
  between operations: 13.4 us -> 0.01 us
    reduce_scatter x1 -> x0, waiting for transfers between devices: 186 us -> none  [local_gram(): lax.psum_scatter(packed_partial(blocks), 'dp', scatter_dimension=0, tiled...]
    pallas_call x0 -> x1, Pallas kernels: none -> 133 us  [local_gram(): pl.pallas_call(functools.partial(_kernel, groups, blk), out_shape=jax.Sha...]
    dot_general x5 -> x0, matrix products: 129 us -> none  [slot_step(): jnp.einsum('gik,gjk->gij', blocks, partner, preferred_element_type=jnp.fl...]
    dynamic_update_slice x5 -> x0, other arithmetic: 50.2 us -> none  [slot_step(): lax.dynamic_update_index_in_dim(packed, jnp.where(keep_mask, flipped, 0.0...]
    dot_general x5 -> x0, local copies, waits for them, and re-layouts: 42.6 us -> none  [slot_step(): jnp.einsum('gik,gjk->gij', blocks, partner, preferred_element_type=jnp.fl...]
    concatenate x1 -> x0, other arithmetic: 38.9 us -> none  [packed_partial(): doubled = jnp.concatenate([blocks, blocks], axis=0)]
    unnamed x0 -> x1, local copies, waits for them, and re-layouts: none -> 5.26 us
  transfers between devices with their start and end apart: 1 -> 0, of which waited for: 1 -> 0; matrix products, arithmetic and copies ran while one was open for 0% -> 0% of each run, Pallas kernels for 0% -> 0%
where the time goes in v1:
time: 139 us; the launch traced here: 138 us
  Pallas kernels  133 us (96%)
  local copies, waits for them, and re-layouts  5.26 us (4%)
    pallas_call x1, Pallas kernels, local_gram(): pl.pallas_call(functools.partial(_kernel, groups, blk), out_shape=jax.Sha...  133 us
    unnamed x1, local copies, waits for them, and re-layouts  5.26 us

profile of v1, /device:TPU:81, one launch (start us, length us, event | category | flops | bytes accessed | tf_op | source)
XLA Modules:
  0.0 138.5 jit_solution(7759000634731239074)
XLA Ops:
  0.0 133.2 %shard_map.17 = f32[5,448,448]{2,1,0:T(8,128)} custom-call(bf16[3584,4096]{1,0:T(8,128)(2,1)} %a_hbm.1), custom_call_target="tpu_custom_call" | custom-call | tf_op jit(solution)/shard_map/pallas_call | solution.py:291
  133.2 5.3 %copy.3 = f32[1,5,448,448]{3,2,1,0:T(8,128)} copy(f32[1,5,448,448]{3,2,1,0:T(8,128)} %bitcast.1) | data formatting | bytes 8028160

commit v2 on v1

--- a/solution.py
+++ b/solution.py
@@ -10,7 +10,34 @@
 CORES = 2
 LANES = 128
 O_SLOTS = 4
+VMEM_BYTES = 67_043_328
 MESH = pl.DeviceIdType.MESH
+
+
+def _diag_rows(blk):
+    return 2 * blk - LANES, LANES + (blk - 2 * LANES) // 2
+
+
+def _ring_rows(groups, blk):
+    rows_dl, rows_ds = _diag_rows(blk)
+    rows_l, rows_s = 2 * blk, blk + blk // 2
+    middle = groups // 2 - 1
+    return max(rows_dl + middle * rows_s + rows_l, rows_ds + middle * rows_l + rows_s)
+
+
+def _store_kernel(src, out, hold, in_sem, out_sem):
+    pieces = [(slot, pl.ds(part * hold.shape[1] // 2, hold.shape[1] // 2)) for slot in range(hold.shape[0]) for part in range(2)]
+    loads = [pltpu.make_async_copy(src.at[slot, rows], hold.at[slot, rows], in_sem.at[n])
+             for n, (slot, rows) in enumerate(pieces)]
+    stores = [pltpu.make_async_copy(hold.at[slot, rows], out.at[slot, rows], out_sem.at[n])
+              for n, (slot, rows) in enumerate(pieces)]
+    for copy in loads:
+        copy.start()
+    for copy_in, copy_out in zip(loads, stores):
+        copy_in.wait()
+        copy_out.start()
+    for copy in stores:
+        copy.wait()
 
 
 def _kernel(groups, blk, a_hbm, out_hbm, a, x, ring, outgoing, acc, stage,
@@ -25,10 +52,9 @@
     mid = blk // 2
     rows_l, rows_s = 2 * blk, blk + mid
     edge = blk - LANES
-    low = blk - wide
-    rows_dl, rows_ds = 2 * blk - LANES, LANES + low // 2
+    rows_dl, rows_ds = _diag_rows(blk)
     blk_rows = rows_l + rows_s
-    ring_rows = half_groups // 2 * blk_rows + rows_l
+    ring_rows = _ring_rows(groups, blk)
     tail = edge - wide
 
     me = lax.axis_index("dp")
@@ -44,10 +70,10 @@
     def load(index):
         return pltpu.make_async_copy(a_hbm.at[row_block(index)], a.at[row_block(index)], load_sem.at[index])
 
-    first = (chip_down * CORES + 1 - core, chip_up * CORES + 1 - core, chip_down * CORES + core, chip_up * CORES + core)
     chip_far = (chip + 2) % chips
-    rest = (chip * CORES + 1 - core, chip * CORES + core, chip_far * CORES + 1 - core, chip_far * CORES + core)
-    for index in first + rest:
+    order = (chip_down * CORES + 1 - core, chip_up * CORES + 1 - core, chip_down * CORES + core, chip_up * CORES + core,
+             chip_far * CORES + 1, chip * CORES + 1, chip_far * CORES, chip * CORES)
+    for index in order[:2]:
         load(index).start()
 
     barrier = pltpu.get_barrier_semaphore()
@@ -58,10 +84,12 @@
     def item(n):
         step = n // per_step
         rest_n = n % per_step
-        slot, way = rest_n // 2, rest_n % 2
+        slot = rest_n // 2
+        way = (rest_n + slot) % 2
+        middle = (slot + groups - 1) // groups - slot // half_groups
         dest = (chip + 2 * chips + (1 + step) * (2 * way - 1)) % chips
         valid = jnp.logical_or(slot < half_groups, dest < chips // 2)
-        return step, slot, way, dest, (slot + way) % 2, valid
+        return step, slot, way, dest, (middle + way) % 2, valid
 
     def by_case(slot, half, fn):
         for diag in (True, False):
@@ -76,9 +104,16 @@
         wrapped = (slot + groups - 1 - p) // groups
         hi = p + wrapped * (q - p)
         lo = q + wrapped * (p - q)
-        left = a[row_block(hi), :]
-        right = a[pl.ds(pl.multiple_of(lo * blk + half * (blk - wide), 64), wide), :]
-        acc[...] = lax.dot_general(left, right, (((1,), (1,)), ((), ())), preferred_element_type=jnp.float32)
+        right = pl.ds(pl.multiple_of(lo * blk + half * (blk - wide), 64), wide)
+        corner = jnp.logical_and(slot == 0, half == 1)
+
+        def product(top):
+            left = pl.ds(pl.multiple_of(hi * blk + top, 64), blk - top)
+            acc[top:, :] = lax.dot_general(a[left, :], a[right, :], (((1,), (1,)), ((), ())),
+                                           preferred_element_type=jnp.float32)
+
+        pl.when(corner)(functools.partial(product, wide))
+        pl.when(jnp.logical_not(corner))(functools.partial(product, 0))
 
     def emit(diag, part, put):
         if part == 0:
@@ -96,7 +131,9 @@
         return pl.multiple_of((dest * slots + slot) * blk_rows + half * rows_l, 32)
 
     def ring_base(step, slot, way):
-        off = (slot // 2) * blk_rows + (slot % 2) * (rows_l + way * (rows_s - rows_l))
+        first_rows = rows_dl + way * (rows_ds - rows_dl)
+        other_rows = rows_s + way * (rows_l - rows_s)
+        off = (slot + groups - 1) // groups * (first_rows + (slot - 1) * other_rows)
         return pl.multiple_of((way * steps + step) * ring_rows + off, 32)
 
     def pair_copy(n, dest, slot, half, rows):
@@ -215,7 +252,7 @@
                 def _():
                     finish(slot, diag, part, value)
 
-            @pl.when(jnp.logical_and(step == steps, jnp.logical_and(way == 0, slot >= 2)))
+            @pl.when(jnp.logical_and(step == steps, jnp.logical_and(n % 2 == 0, slot >= 2)))
             def _():
                 out_copy(slot - 2).wait()
 
@@ -223,28 +260,37 @@
 
         @pl.when(jnp.logical_and(step == steps, jnp.logical_not(valid)))
         def _():
-            @pl.when(way == 0)
+            @pl.when(n % 2 == 0)
             def _():
                 out_copy(slot - 2).wait()
                 stage[slot % 2] = jnp.zeros(stage.shape[1:], stage.dtype)
 
-        @pl.when(jnp.logical_and(step == steps, way == 1))
+        @pl.when(jnp.logical_and(step == steps, n % 2 == 1))
         def _():
             out_copy(slot).start()
 
-    load(first[0]).wait()
-    for_partner(0)
+    def ready(*places):
+        for place in places:
+            load(order[place]).wait()
+            if place + 2 < groups:
+                load(order[place + 2]).start()
 
     def body(n, carry):
+        @pl.when(n == -1)
+        def _():
+            ready(0)
+
         @pl.when(n == 0)
         def _():
-            load(first[1]).wait()
+            ready(1)
 
         @pl.when(n == 1)
         def _():
-            load(first[3]).wait()
-            for index in rest:
-                load(index).wait()
+            ready(3, 4, 5)
+
+        @pl.when(n == 3)
+        def _():
+            ready(6, 7)
 
         @pl.when(n + 1 < n_items)
         def _():
@@ -252,12 +298,15 @@
 
         @pl.when(n == 0)
         def _():
-            load(first[2]).wait()
-
-        for_me(n)
+            ready(2)
+
+        @pl.when(n >= 0)
+        def _():
+            for_me(n)
+
         return carry
 
-    lax.fori_loop(0, n_items, body, 0)
+    lax.fori_loop(-1, n_items, body, 0)
 
     def drain(n, carry):
         step, slot, way, dest, half, valid = item(n)
@@ -283,12 +332,12 @@
     def local_gram(a_local):
         n_rows, local_cols = a_local.shape
         blk = n_rows // groups
-        rows_l, rows_s = 2 * blk, blk + blk // 2
-        blk_rows = rows_l + rows_s
-        ring_rows = groups // 4 * blk_rows + rows_l
+        rows_l = 2 * blk
+        blk_rows = 3 * blk + blk // 2
+        ring_rows = _ring_rows(groups, blk)
         n_items = chips * 2 * slots
         n_ring = 2 * (chips - 1) * slots
-        return pl.pallas_call(
+        blocks = pl.pallas_call(
             functools.partial(_kernel, groups, blk),
             out_shape=jax.ShapeDtypeStruct((slots, blk, blk), jnp.float32),
             in_specs=[pl.BlockSpec(memory_space=pl.ANY)],
@@ -308,7 +357,20 @@
                 pltpu.SemaphoreType.DMA((2,)),
             ],
             compiler_params=pltpu.CompilerParams(
-                collective_id=0, has_side_effects=True, vmem_limit_bytes=67_043_328),
-        )(a_local)[None]
+                collective_id=0, has_side_effects=True, vmem_limit_bytes=VMEM_BYTES),
+        )(a_local)
+        stored = pl.pallas_call(
+            _store_kernel,
+            out_shape=jax.ShapeDtypeStruct(blocks.shape, blocks.dtype),
+            in_specs=[pl.BlockSpec(memory_space=pl.ANY)],
+            out_specs=pl.BlockSpec(memory_space=pl.ANY),
+            scratch_shapes=[
+                pltpu.VMEM(blocks.shape, blocks.dtype),
+                pltpu.SemaphoreType.DMA((2 * slots,)),
+                pltpu.SemaphoreType.DMA((2 * slots,)),
+            ],
+            compiler_params=pltpu.CompilerParams(vmem_limit_bytes=VMEM_BYTES),
+        )(blocks)
+        return stored[None]
 
     return jax.shard_map(local_gram, mesh=mesh, in_specs=(P("mat", "dp"),), out_specs=P(("mat", "dp")), check_vma=False)

time: 139 us -> 132 us (0.950)
  local copies, waits for them, and re-layouts: 5.26 us -> 0 us
  Pallas kernels: 133 us -> 131 us
    pallas_call x1, Pallas kernels: 133 us -> 127 us  [local_gram(): pl.pallas_call(functools.partial(_kernel, groups, blk), out_shape=jax.Sha...]
    unnamed x1 -> x0, local copies, waits for them, and re-layouts: 5.26 us -> none
    pallas_call x0 -> x1, Pallas kernels: none -> 4.06 us  [local_gram(): pl.pallas_call(_store_kernel, out_shape=jax.ShapeDtypeStruct(blocks.shape...]
where the time goes in v2:
time: 132 us; the launch traced here: 131 us
  Pallas kernels  131 us (99%)
    pallas_call x1, Pallas kernels, local_gram(): pl.pallas_call(functools.partial(_kernel, groups, blk), out_shape=jax.Sha...  127 us
    pallas_call x1, Pallas kernels, local_gram(): pl.pallas_call(_store_kernel, out_shape=jax.ShapeDtypeStruct(blocks.shape...  4.06 us

profile of v2, /device:TPU:81, one launch (start us, length us, event | category | flops | bytes accessed | tf_op | source)
XLA Modules:
  0.0 131.4 jit_solution(12230585021540048164)
XLA Ops:
  0.0 127.3 %shard_map.17.src = f32[5,448,448]{2,1,0:T(8,128)} custom-call(bf16[3584,4096]{1,0:T(8,128)(2,1)} %a_hbm.1), custom_call_target="tpu_custom_call" | custom-call | tf_op jit(solution)/shard_map/pallas_call | solution.py:340
  127.3 4.1 %shard_map.18 = f32[5,448,448]{2,1,0:T(8,128)} custom-call(f32[5,448,448]{2,1,0:T(8,128)} %shard_map.17.src), custom_call_target="tpu_custom_call" | custom-call | tf_op jit(solution)/shard_map/pallas_call | solution.py:362

commit v3 on v2

v3 whole, which is shorter than its diff:
```python
import functools

import jax
import jax.numpy as jnp
from jax import lax
from jax.experimental import pallas as pl
from jax.experimental.pallas import tpu as pltpu
from jax.sharding import PartitionSpec as P

CORES = 2
LANES = 128
O_SLOTS = 4
VMEM_BYTES = 67_043_328
MESH = pl.DeviceIdType.MESH


class _Pieces:
    HEAD, SIDE, CORNER, LEFT, RIGHT = range(5)

    def __init__(self, groups, blk):
        wide = 2 * LANES
        low = blk - wide
        self.rows = (wide + LANES, 2 * low, LANES + low // 2, 2 * blk, blk + blk // 2)
        self.block = self.rows[self.LEFT] + self.rows[self.RIGHT]
        self.at = (0, self.rows[self.HEAD], self.rows[self.LEFT], 0, self.rows[self.LEFT])
        half = groups // 2
        self.slots = half + 1
        middle = half - 1
        self.ways = (
            [self.HEAD, self.SIDE] + [self.RIGHT] * middle + [self.LEFT],
            [self.CORNER] + [self.LEFT] * middle + [self.RIGHT],
        )
        self.places = len(self.ways[0])
        self.ring = max(sum(self.rows[kind] for kind in way) for way in self.ways)


def _store_kernel(src, out, hold, in_sem, out_sem):
    pieces = [(slot, pl.ds(part * hold.shape[1] // 2, hold.shape[1] // 2)) for slot in range(hold.shape[0]) for part in range(2)]
    loads = [pltpu.make_async_copy(src.at[slot, rows], hold.at[slot, rows], in_sem.at[n])
             for n, (slot, rows) in enumerate(pieces)]
    stores = [pltpu.make_async_copy(hold.at[slot, rows], out.at[slot, rows], out_sem.at[n])
              for n, (slot, rows) in enumerate(pieces)]
    for copy in loads:
        copy.start()
    for copy_in, copy_out in zip(loads, stores):
        copy_in.wait()
        copy_out.start()
    for copy in stores:
        copy.wait()


def _kernel(groups, blk, a_hbm, out_hbm, a, x, ring, outgoing, acc, stage,
            load_sem, pair_send, pair_recv, ring_send, ring_recv, out_sem):
    pieces = _Pieces(groups, blk)
    HEAD, SIDE, CORNER, LEFT, RIGHT = range(5)
    chips = groups // CORES
    half_groups = groups // 2
    slots, places = pieces.slots, pieces.places
    steps = chips - 1
    per_step = 2 * places
    n_items = chips * per_step
    wide = 2 * LANES
    edge = blk - LANES
    tail = edge - wide
    low = blk - wide
    mid = blk // 2
    rows_l = pieces.rows[LEFT]

    me = lax.axis_index("dp")
    chip, core = me // CORES, me % CORES
    partner = chip * CORES + 1 - core
    chip_up = (chip + 1) % chips
    chip_down = (chip + chips - 1) % chips
    chip_far = (chip + 2) % chips
    up, down = chip_up * CORES + core, chip_down * CORES + core

    cuts = (0, wide - tail, wide, blk)

    def load(index, parts):
        begin, end = cuts[parts[0]], cuts[parts[-1] + 1]
        rows = pl.ds(pl.multiple_of(index * blk + begin, 64), end - begin)
        return pltpu.make_async_copy(a_hbm.at[rows], a.at[rows], load_sem.at[index, parts[0]])

    whole, top, strip, bottom = (0, 1, 2), (0,), (1,), (2,)
    down_other, down_same = chip_down * CORES + 1 - core, chip_down * CORES + core
    up_other, up_same = chip_up * CORES + 1 - core, chip_up * CORES + core
    loads = (
        [load(down_other, top), load(down_other, strip)],
        [load(up_other, strip), load(up_other, bottom)],
        [load(down_same, top), load(down_same, strip)],
        [load(up_same, strip), load(up_same, bottom)],
        [load(up_other, top), load(up_same, top), load(chip * CORES + 1, whole)],
        [load(down_other, bottom)],
        [load(down_same, bottom)],
        [load(chip_far * CORES + 1, whole)],
        [load(chip * CORES, whole)],
        [load(chip_far * CORES, whole)],
    )
    for batch in loads:
        for copy in batch:
            copy.start()

    def ready(n, batches):
        for at, batch in batches.items():
            @pl.when(n == at)
            def _(batch=batch):
                for copy in loads[batch]:
                    copy.wait()

    ready_partner = functools.partial(ready, batches={0: 0, 1: 1, 2: 4, 3: 5, 4: 7, 5: 8, 6: 9})
    ready_mine = functools.partial(ready, batches={0: 2, 1: 3, 3: 6})

    barrier = pltpu.get_barrier_semaphore()
    for other in (partner, up, down):
        pl.semaphore_signal(barrier, inc=1, device_id={"dp": other}, device_id_type=MESH)
    pl.semaphore_wait(barrier, 3)

    def item(n):
        step = n // per_step
        place = n % per_step // 2
        way = (n + place) % 2
        dest = (chip + 2 * chips + (1 + step) * (2 * way - 1)) % chips
        after = (place + places - 1) // places
        slot = place - (1 - way) * after
        in_table = jnp.logical_or(way == 0, place < places - 1)
        valid = jnp.logical_and(in_table, jnp.logical_or(slot < half_groups, dest < chips // 2))
        return step, place, way, dest, slot, valid

    def by_case(place, way, fn):
        cases = {}
        for table_way, kinds in enumerate(pieces.ways):
            for at, kind in enumerate(kinds):
                cases.setdefault(kind, []).append((table_way, at))
        for kind, spots in cases.items():
            cond = False
            for table_way in (0, 1):
                ats = [at for w, at in spots if w == table_way]
                if ats:
                    hit = jnp.logical_and(way == table_way, jnp.logical_and(place >= min(ats), place <= max(ats)))
                    cond = hit if cond is False else jnp.logical_or(cond, hit)
            pl.when(cond)(functools.partial(fn, kind))

    def multiply(dest, parity, slot, place, way):
        p = dest * CORES + parity
        q = (p - slot + groups) % groups
        wrapped = (slot + groups - 1 - p) // groups
        hi = p + wrapped * (q - p)
        lo = q + wrapped * (p - q)

        def product(begin, end, shift):
            left = pl.ds(pl.multiple_of(hi * blk + begin, 64), end - begin)
            right = pl.ds(pl.multiple_of(lo * blk + shift, 64), wide)
            acc[begin:end, :] = lax.dot_general(a[left, :], a[right, :], (((1,), (1,)), ((), ())),
                                                preferred_element_type=jnp.float32)

        head = jnp.logical_and(slot == 0, jnp.logical_and(way == 0, place == 0))
        below = jnp.logical_and(slot == 0, jnp.logical_not(head))
        last = (place + 1) // places
        right_half = jnp.where(way == 0, 1 - last, place // (places - 2))
        pl.when(head)(functools.partial(product, 0, wide, 0))
        pl.when(below)(functools.partial(product, wide, blk, way * low))
        pl.when(slot > 0)(functools.partial(product, 0, blk, right_half * low))

    lane_of = lambda n: lax.broadcasted_iota(jnp.int32, (n, LANES), 1)

    def emit(kind, put):
        if kind in (HEAD, SIDE, LEFT):
            begin, end = {HEAD: (0, wide), SIDE: (wide, blk), LEFT: (0, blk)}[kind]
            put(0, acc[begin:end, :LANES])
            put(end - begin, acc[LANES if kind == HEAD else begin:end, LANES:])
        else:
            begin = wide if kind == CORNER else 0
            cut = (begin + blk) // 2
            full = edge if kind == CORNER else 0
            put(0, acc[full:, LANES:])
            put(blk - full, jnp.where(lane_of(blk - cut) < tail, pltpu.roll(acc[begin:cut, :LANES], tail, 1), acc[cut:, :LANES]))

    def spot(kind, place):
        kinds = pieces.ways[0 if kind in (HEAD, SIDE) else 1]
        if kind in (HEAD, SIDE, CORNER):
            return sum(pieces.rows[k] for k in kinds[:kinds.index(kind)])
        return None

    def x_base(kind, dest, slot):
        return pl.multiple_of((dest * slots + slot) * pieces.block + pieces.at[kind], 32)

    def ring_base(kind, step, place, way):
        if spot(kind, place) is not None:
            off = spot(kind, place)
        else:
            size = pieces.rows
            up_off = size[HEAD] + size[SIDE] + (place - 2) * size[RIGHT]
            down_off = size[CORNER] + (place - 1) * size[LEFT]
            off = up_off + way * (down_off - up_off)
        return pl.multiple_of((way * steps + step) * pieces.ring + off, 32)

    def pair_copy(kind, n, dest, slot):
        rows = pieces.rows[kind]
        return pltpu.make_async_remote_copy(
            src_ref=outgoing.at[pl.ds(pl.multiple_of((n % O_SLOTS) * rows_l, 32), rows)],
            dst_ref=x.at[pl.ds(x_base(kind, dest, slot), rows)],
            send_sem=pair_send.at[n], recv_sem=pair_recv.at[n],
            device_id={"dp": partner}, device_id_type=MESH)

    def ring_copy(kind, step, place, way, dest, slot):
        rows = pieces.rows[kind]
        target = up + way * (down - up)
        sem = (way * steps + step) * places + place
        return pltpu.make_async_remote_copy(
            src_ref=x.at[pl.ds(x_base(kind, dest, slot), rows)],
            dst_ref=ring.at[pl.ds(ring_base(kind, step, place, way), rows)],
            send_sem=ring_send.at[sem], recv_sem=ring_recv.at[sem],
            device_id={"dp": target}, device_id_type=MESH)

    def wait_pair_send(n):
        _, place, way, dest, slot, valid = item(n)

        @pl.when(valid)
        def _():
            by_case(place, way, lambda kind: pair_copy(kind, n, dest, slot).wait_send())

    def for_partner(n):
        _, place, way, dest, slot, valid = item(n)

        @pl.when(n >= O_SLOTS)
        def _():
            wait_pair_send(n - O_SLOTS)

        @pl.when(valid)
        def _():
            multiply(dest, 1 - core, slot, place, way)
            base = (n % O_SLOTS) * rows_l

            def send(kind):
                def put(row, value):
                    outgoing[pl.ds(pl.multiple_of(base + row, 32), value.shape[0]), :] = value

                emit(kind, put)
                pair_copy(kind, n, dest, slot).start()

            by_case(place, way, send)

    def out_copy(slot):
        return pltpu.make_async_copy(stage.at[slot % 2], out_hbm.at[slot], out_sem.at[slot % 2])

    def finish(kind, slot, value):
        block = stage.at[slot % 2]
        if kind == LEFT:
            block[:, :LANES] = value(0, blk)
            block[:, LANES:wide] = value(blk, blk)
        elif kind == HEAD:
            col0 = value(0, wide)
            block[:wide, :LANES] = col0
            block[LANES:wide, LANES:wide] = value(wide, LANES)
            block[:LANES, LANES:wide] = col0[LANES:].T
        elif kind == SIDE:
            for part in (0, 1):
                col = value(part * low, low)
                lanes = slice(part * LANES, (part + 1) * LANES)
                block[wide:, lanes] = col
                block[lanes, wide:wide + LANES] = col[:LANES].T
                block[lanes, wide + LANES:] = col[LANES:].T
        else:
            begin = wide if kind == CORNER else 0
            full = LANES if kind == CORNER else blk
            cut = (blk - begin) // 2
            tile = value(0, full)
            packed = value(full, cut)
            rolled = pltpu.roll(packed, tail, 1)
            if kind == CORNER:
                across = jnp.concatenate([packed[tail:], rolled], axis=0)[:, :tail].T
                tile = jnp.concatenate([across, tile], axis=0)
            tile = pltpu.roll(tile, tail, 1)
            lane = lane_of(cut)
            block[begin:begin + cut, wide:3 * LANES] = jnp.where(lane < tail, packed, tile[:cut])
            block[begin + cut:, wide:3 * LANES] = jnp.where(lane < tail, rolled, tile[cut:])
            block[begin:, 3 * LANES:] = tile[:, :tail]

    def for_me(n):
        step, place, way, dest, slot, valid = item(n)
        final = step == steps

        @pl.when(jnp.logical_and(final, jnp.logical_and(way == 1, jnp.logical_and(place >= 2, place < slots))))
        def _():
            out_copy(place - 2).wait()

        @pl.when(valid)
        def _():
            multiply(dest, core, slot, place, way)

            def add(kind):
                rows = pieces.rows[kind]
                base = x_base(kind, dest, slot)
                pair_copy(kind, n, dest, slot).wait_recv()

                def put(row, value):
                    span = pl.ds(pl.multiple_of(base + row, 32), value.shape[0])
                    x[span, :] = x[span, :] + value

                emit(kind, put)

                @pl.when(step > 0)
                def _():
                    ring_copy(kind, step - 1, place, way, dest, slot).wait_recv()

                r_base = ring_base(kind, step - 1, place, way)

                def value(row, size):
                    return (x[pl.ds(pl.multiple_of(base + row, 32), size), :]
                            + ring[pl.ds(pl.multiple_of(r_base + row, 32), size), :])

                @pl.when(jnp.logical_and(step > 0, step < steps))
                def _():
                    x[pl.ds(base, rows), :] = value(0, rows)

                @pl.when(step < steps)
                def _():
                    ring_copy(kind, step, place, way, dest, slot).start()

                @pl.when(final)
                def _():
                    finish(kind, slot, value)

            by_case(place, way, add)

        @pl.when(jnp.logical_and(final, jnp.logical_and(way == 0, place >= 1)))
        def _():
            @pl.when(jnp.logical_not(valid))
            def _():
                stage[slot % 2] = jnp.zeros(stage.shape[1:], stage.dtype)

            out_copy(slot).start()

    def pair(index, carry):
        def partner_item(turn, inner):
            ready_partner(2 * index + turn)
            for_partner(2 * index + turn)
            return inner

        def my_item(turn, inner):
            ready_mine(2 * index + turn)
            for_me(2 * index + turn)
            return inner

        lax.fori_loop(0, 2, partner_item, 0)
        lax.fori_loop(0, 2, my_item, 0)
        return carry

    lax.fori_loop(0, n_items // 2, pair, 0)

    def drain(n, carry):
        step, place, way, dest, slot, valid = item(n)

        @pl.when(valid)
        def _():
            by_case(place, way, lambda kind: ring_copy(kind, step, place, way, dest, slot).wait_send())

        return carry

    lax.fori_loop(0, steps * per_step, drain, 0)
    for n in range(n_items - O_SLOTS, n_items):
        wait_pair_send(n)
    for slot in (slots - 2, slots - 1):
        out_copy(slot).wait()


def solution(mesh):
    groups = mesh.shape["dp"]
    chips = groups // CORES

    def local_gram(a_local):
        n_rows, local_cols = a_local.shape
        blk = n_rows // groups
        pieces = _Pieces(groups, blk)
        slots = pieces.slots
        n_items = chips * 2 * pieces.places
        n_ring = 2 * (chips - 1) * pieces.places
        blocks = pl.pallas_call(
            functools.partial(_kernel, groups, blk),
            out_shape=jax.ShapeDtypeStruct((slots, blk, blk), jnp.float32),
            in_specs=[pl.BlockSpec(memory_space=pl.ANY)],
            out_specs=pl.BlockSpec(memory_space=pl.ANY),
            scratch_shapes=[
                pltpu.VMEM((n_rows, local_cols), jnp.bfloat16),
                pltpu.VMEM((chips * slots * pieces.block, LANES), jnp.float32),
                pltpu.VMEM((2 * (chips - 1) * pieces.ring, LANES), jnp.float32),
                pltpu.VMEM((O_SLOTS * pieces.rows[pieces.LEFT], LANES), jnp.float32),
                pltpu.VMEM((blk, 2 * LANES), jnp.float32),
                pltpu.VMEM((2, blk, blk), jnp.float32),
                pltpu.SemaphoreType.DMA((groups, 3)),
                pltpu.SemaphoreType.DMA((n_items,)),
                pltpu.SemaphoreType.DMA((n_items,)),
                pltpu.SemaphoreType.DMA((n_ring,)),
                pltpu.SemaphoreType.DMA((n_ring,)),
                pltpu.SemaphoreType.DMA((2,)),
            ],
            compiler_params=pltpu.CompilerParams(
                collective_id=0, has_side_effects=True, vmem_limit_bytes=VMEM_BYTES),
        )(a_local)
        stored = pl.pallas_call(
            _store_kernel,
            out_shape=jax.ShapeDtypeStruct(blocks.shape, blocks.dtype),
            in_specs=[pl.BlockSpec(memory_space=pl.ANY)],
            out_specs=pl.BlockSpec(memory_space=pl.ANY),
            scratch_shapes=[
                pltpu.VMEM(blocks.shape, blocks.dtype),
                pltpu.SemaphoreType.DMA((2 * slots,)),
                pltpu.SemaphoreType.DMA((2 * slots,)),
            ],
            compiler_params=pltpu.CompilerParams(vmem_limit_bytes=VMEM_BYTES),
        )(blocks)
        return stored[None]

    return jax.shard_map(local_gram, mesh=mesh, in_specs=(P("mat", "dp"),), out_specs=P(("mat", "dp")), check_vma=False)
```

time: 132 us -> 133 us (level)
  the two profiles are of different devices: /device:TPU:81 before, /device:TPU:125 now
where the time goes in v3:
time: 133 us
  Pallas kernels  133 us (100%)
    pallas_call x1, Pallas kernels, local_gram(): pl.pallas_call(functools.partial(_kernel, groups, blk), out_shape=jax.Sha...  129 us
    pallas_call x1, Pallas kernels, local_gram(): pl.pallas_call(_store_kernel, out_shape=jax.ShapeDtypeStruct(blocks.shape...  4.06 us

profile of v3, /device:TPU:125, one launch (start us, length us, event | category | flops | bytes accessed | tf_op | source)
XLA Modules:
  0.0 133.1 jit_solution(15369494587402205243)
XLA Ops:
  0.0 129.0 %shard_map.17.src = f32[5,448,448]{2,1,0:T(8,128)} custom-call(bf16[3584,4096]{1,0:T(8,128)(2,1)} %a_hbm.1), custom_call_target="tpu_custom_call" | custom-call | tf_op jit(solution)/shard_map/pallas_call | solution.py:378
  129.0 4.1 %shard_map.18 = f32[5,448,448]{2,1,0:T(8,128)} custom-call(f32[5,448,448]{2,1,0:T(8,128)} %shard_map.17.src), custom_call_target="tpu_custom_call" | custom-call | tf_op jit(solution)/shard_map/pallas_call | solution.py:400
